TPU v7x, 32 devices: a whole 2x2x4 slice. The times are simulated.
32 devices in a mesh: section: 4 (over z), shard: 8 (over y, x, core).
Axes of the slice: x: 2, y: 2, z: 4, core: 2. Of those that a mesh axis runs over, the one named last changes fastest.
Arguments:
- grad_parts: bfloat16 [4, 8, 256, 8192], P('section', 'shard'), may hold values from -6 to 6
- params: bfloat16 [4, 256, 8192], P('section', 'shard'), may hold values from -6 to 6
- moment_first: float32 [4, 256, 8192], P('section', 'shard'), may hold values from -6 to 6
- moment_second: float32 [4, 256, 8192], P('section', 'shard'), may hold values from 0.5 to 50
- block_layer: int32 [4, 32], P('section', 'shard'), may hold values from 0 to 7, as said below
- block_valid: int32 [4, 32], P('section', 'shard'), may hold values from 0 to 1
- decay: float32 [8], replicated, may hold values from 0.05 to 1
Outputs:
- new_params: bfloat16 [4, 256, 8192], P('section', 'shard')
- new_first: float32 [4, 256, 8192], P('section', 'shard')
- new_second: float32 [4, 256, 8192], P('section', 'shard')
- ratios: float32 [8], replicated
Inputs may be any that keep to these rules, and one draw needn't show every extreme that they name: `block_layer`: in every section the live slots come first. One section has all 32 slots live; each other section has between 16 and 32 live slots, and all sections together have 3 * 32. Over the live slots taken section by section in order, layer ids never fall and every layer has exactly 12 live slots; dead slots hold arbitrary layer ids.
All inputs are finite; a program needn't handle non-finite values.
Results may differ from a plain program's by a relative error of at most 0.008.
Values may be sent and summed in bfloat16 or wider, within the bound.
A program may use at most 64 MiB of HBM per device.

v0:
```python
import jax
import jax.numpy as jnp
from jax import lax
from jax.sharding import PartitionSpec as P

bias_first = 1.0 - 0.9**10
bias_second = 1.0 - 0.99**10


def carried_in(part, axis, combine, identity):
    place = lax.axis_index(axis)
    gathered = lax.all_gather(part, axis)
    state = jnp.zeros_like(part) + jnp.asarray(identity, part.dtype)

    def one(step, state):
        return combine(state, lax.dynamic_index_in_dim(gathered, step, 0, False))

    return lax.fori_loop(0, place, one, state)


def from_root(block, axis, source):
    block = jnp.where(lax.axis_index(axis) == source, block, jnp.zeros_like(block))
    return lax.psum(block, axis)


def combine_sum(earlier, later):
    return earlier + later


def shards(grad_parts, params, moment_first, moment_second, block_layer, block_valid, decay):
    row_count = params.shape[1]
    local_grad = grad_parts[0, 0]
    gradient = lax.psum_scatter(
        local_grad.astype(jnp.float32).astype(jnp.bfloat16),
        "shard",
        scatter_dimension=0,
        tiled=True,
    ).astype(jnp.float32)
    block_rows = row_count // block_layer.shape[1]
    layer_rows = jnp.repeat(block_layer[0], block_rows)
    valid_rows = jnp.repeat(block_valid[0], block_rows) > 0
    layer_ids = jnp.arange(decay.shape[0], dtype=jnp.int32)
    onehot = jnp.where(
        valid_rows[:, None] & (layer_rows[:, None] == layer_ids[None, :]), 1.0, 0.0
    ).astype(jnp.float32)
    weights = params[0].astype(jnp.float32)
    first = 0.9 * moment_first[0] + 0.1 * gradient
    second = 0.99 * moment_second[0] + 0.01 * gradient * gradient
    row_decay = jnp.dot(onehot, decay, precision=lax.Precision.HIGHEST)
    update = (
        first / bias_first / (jnp.sqrt(second / bias_second) + 1e-06) + row_decay[:, None] * weights
    )
    row_sums = jnp.stack(
        [jnp.sum(weights * weights, axis=-1), jnp.sum(update * update, axis=-1)], axis=1
    )
    partial_value = jnp.dot(onehot.T, row_sums, precision=lax.Precision.HIGHEST)
    section_total = lax.psum(partial_value, "shard")
    before = carried_in(section_total, "section", combine_sum, jnp.zeros_like(section_total))
    through = before + section_total
    totals = from_root(through, "section", lax.axis_size("section") - 1)
    ratios = jnp.sqrt(totals[:, 0] / (totals[:, 1] + 1.0))
    row_ratio = jnp.dot(onehot, ratios, precision=lax.Precision.HIGHEST)
    stepped = weights - 0.1 * row_ratio[:, None] * update
    live = valid_rows[:, None]
    new_params = jnp.where(live, stepped, weights).astype(jnp.bfloat16)
    new_first = jnp.where(live, first, moment_first[0])
    new_second = jnp.where(live, second, moment_second[0])
    return (new_params[None], new_first[None], new_second[None], ratios)


def solution(mesh):
    placed = (
        P("section", "shard", None, None),
        P("section", "shard", None),
        P("section", "shard", None),
        P("section", "shard", None),
        P("section", "shard"),
        P("section", "shard"),
        P(),
    )
    return jax.shard_map(
        shards,
        mesh=mesh,
        in_specs=placed,
        out_specs=(
            P("section", "shard", None),
            P("section", "shard", None),
            P("section", "shard", None),
            P(),
        ),
        check_vma=False,
    )
```

profile of v0, /device:TPU:0, one launch (start us, length us, event | category | flops | bytes accessed | tf_op | source)
XLA Modules:
  0.0 109.7 jit_solution(5550758126043738490)
XLA Ops:
  7.2 0.0 copy-start
  7.2 0.0 copy-start.4
  7.2 0.0 copy-start.3
  7.2 0.0 copy-start.1
  7.2 0.0 copy-start.2
  7.2 0.0 reduce-scatter.2.cloned.1.call-start
  7.3 0.7 reduce-scatter.2.cloned.1.call-update
  8.0 0.0 copy-done.4
  8.0 0.1 broadcast_in_dim.42
  8.1 0.1 gt.20
  8.1 0.0 copy-done.3
  8.1 0.1 broadcast_in_dim.44
  8.2 0.1 eq.18
  8.3 0.0 copy-done
  8.3 0.2 convolution_bitcast_fusion.1
  8.5 56.8 %reduce-scatter.2.cloned.1.call-done = bf16[32,8192]{1,0:T(8,128)(2,1)} async-done(((bf16[256,8192]{1,0:T(8,128)(2,1)}), bf16[32,8192]{1,0:T(8,128)(2,1)}) %reduce-scatter.2.cloned.1.call-update) | async-done | bytes 524304 | tf_op jit(solution)/shard_map/reduce_scatter | solution.py:33
  65.3 0.0 copy-done.1
  65.3 0.0 copy-done.2
  65.3 3.8 %multiply_reduce_fusion = (f32[32]{0:T(128)S(1)}, f32[32,8192]{1,0:T(8,128)S(1)}, f32[1,32,8192]{2,1,0:T(8,128)}, f32[1,32,8192]{2,1,0:T(8,128)}, f32[32]{0:T(128)S(1)}) fusion(bf16[1,32,8192]{2,1,0:T(8,128)(2,1)S(1)} %copy-done.1, f32[32]{0:T(128)S(1)} %convolution_bitcast_fusion.1, f32[1,32,8192]{2,1,0:T(8,128)S(1)} %copy-done.2, ...), kind=kLoop, calls=%fused_computation.26 | loop fusion | flops 5504960 | bytes 6291872 | tf_op jit(solution)/shard_map/reduce_sum | solution.py:54
  69.1 0.2 fusion.15
  69.3 12.5 %psum.14 = f32[8,2]{0,1:T(2,128)S(1)} all-reduce(f32[8,2]{0,1:T(2,128)S(1)} %fusion.15), channel_id=1, replica_groups=mesh['section'=4,'shard'=8] {'shard'}, use_global_device_ids=true, to_apply=%region_3.4 | all-reduce | flops 16 | bytes 128 | tf_op jit(solution)/shard_map/psum | solution.py:57
  81.8 10.9 %all-gather.1 = f32[4,8,2]{1,2,0:T(2,128)S(1)} all-gather(f32[1,8,2]{1,2,0:T(2,128)S(1)} %bitcast.70), channel_id=2, replica_groups=mesh['section'=4,'shard'=8] {'section'}, dimensions={0}, use_global_device_ids=true | all-gather | bytes 320 | tf_op jit(solution)/shard_map/all_gather | solution.py:12
  92.7 8.4 %psum.15 = f32[8,2]{0,1:T(2,128)S(1)} all-reduce(f32[8,2]{0,1:T(2,128)S(1)} %add_select_fusion), channel_id=1, replica_groups=mesh['section'=4,'shard'=8] {'section'}, use_global_device_ids=true, to_apply=%region_6.7 | all-reduce | flops 16 | bytes 128 | tf_op jit(solution)/shard_map/psum | solution.py:23
  101.1 0.2 fusion
  101.3 0.5 fusion.48
  101.8 1.0 fusion.13
  (4 shorter events, 0.0 us)
Async XLA Ops:
  7.2 1.1 %copy-start = (f32[8]{0:T(128)S(1)}, f32[8]{0:T(128)}, u32[]{:S(2)}) copy-start(f32[8]{0:T(128)} %param.15) | copy-start | bytes 100
  7.2 0.8 copy-start.4
  7.2 1.0 copy-start.3
  7.2 58.1 %copy-start.1 = (bf16[1,32,8192]{2,1,0:T(8,128)(2,1)S(1)}, bf16[1,32,8192]{2,1,0:T(8,128)(2,1)}, u32[]{:S(2)}) copy-start(bf16[1,32,8192]{2,1,0:T(8,128)(2,1)} %param.10) | copy-start | bytes 1572868
  7.2 58.1 %copy-start.2 = (f32[1,32,8192]{2,1,0:T(8,128)S(1)}, f32[1,32,8192]{2,1,0:T(8,128)}, u32[]{:S(2)}) copy-start(f32[1,32,8192]{2,1,0:T(8,128)} %param.12) | copy-start | bytes 3145732
  7.2 58.1 %reduce-scatter.2.cloned.1.call-start = ((), (), s32[]{:S(2)}) async-start(), calls=%async_computation.1 | async-start | bytes 4718592 | tf_op jit(solution)/shard_map/reduce_scatter | solution.py:33
Sparse Core Ops, SparseCore 0:
  11.4 53.8 reduce-scatter.1
where the time goes:
time: 110 us
  waiting for transfers between devices  57.5 us (52%)
  blocking collectives  31.8 us (29%)
  between operations  14.1 us (13%)
  other arithmetic  5.4 us (5%)
    reduce_scatter x1, waiting for transfers between devices, shards(): lax.psum_scatter(local_grad.astype(jnp.float32).astype(jnp.bfloat16), 'sh...  56.8 us
    psum x1, blocking collectives, shards(): section_total = lax.psum(partial_value, 'shard')  12.5 us
    all_gather x1, blocking collectives, carried_in(): gathered = lax.all_gather(part, axis)  10.9 us
    psum x1, blocking collectives, from_root(): return lax.psum(block, axis)  8.37 us
    reduce_sum x1, other arithmetic, shards(): jnp.sum(update * update, axis=-1)  3.8 us
  transfers between devices with their start and end apart: 1, of which 1 were waited for; matrix products, arithmetic and copies ran while one was open for 0% of the time, Pallas kernels for 0%

commit v1 on v0

v1 whole, which is shorter than its diff:
```python
import functools
import math

import jax
import jax.numpy as jnp
from jax import lax
from jax.experimental import pallas as pl
from jax.experimental.pallas import tpu as pltpu
from jax.sharding import PartitionSpec as P

MESH = pl.DeviceIdType.MESH
bias_first = 1.0 - 0.9**10
bias_second = 1.0 - 0.99**10
LANES = 128
PIECES = 8


def kernel(
    n_sec, n_y, n_x, pieces,
    g_hbm, p_hbm, m1_hbm, m2_hbm, layer_ref, valid_ref, decay_ref,
    newp_ref, new1_ref, new2_ref, ratio_ref,
    own, away, d2d, p_v, m1_v, m2_v, upd, r1a, r1b, s1a, s1b, r2a, r2b, tiles, ztiles,
    load_sem, state_sem, pair_sem, one_send, one_recv, two_send, two_recv,
    t_send, t_recv, z_send, z_recv,
):
    rows, cols = p_v.shape
    width = cols // pieces
    n_shard = 2 * n_y * n_x
    sec, me = lax.axis_index("section"), lax.axis_index("shard")
    core = lax.rem(me, 2)
    x = lax.rem(me // 2, n_x)
    y = me // (2 * n_x)
    blocks = layer_ref.shape[1]
    block_rows = rows // blocks

    def at(yy, xx, cc):
        return (sec, (yy * n_x + xx) * 2 + cc)

    def span(p):
        return pl.ds(p * width, width)

    loads = []
    for p in range(pieces):
        a = pltpu.make_async_copy(g_hbm.at[:, :, 1 - core, :, span(p)], away.at[:, :, :, span(p)], load_sem.at[0, p])
        b = pltpu.make_async_copy(g_hbm.at[:, :, core, :, span(p)], own.at[:, :, :, span(p)], load_sem.at[1, p])
        a.start()
        b.start()
        loads.append((a, b))
    states = [
        pltpu.make_async_copy(src, dst, state_sem.at[i])
        for i, (src, dst) in enumerate(((p_hbm, p_v), (m1_hbm, m1_v), (m2_hbm, m2_v)))
    ]
    for s in states:
        s.start()

    barrier = pltpu.get_barrier_semaphore()
    for j in range(1, n_shard):
        pl.semaphore_signal(barrier, inc=1, device_id=(sec, lax.rem(me + j, n_shard)), device_id_type=MESH)
    for j in range(1, n_sec):
        pl.semaphore_signal(barrier, inc=1, device_id=(lax.rem(sec + j, n_sec), me), device_id_type=MESH)
    pl.semaphore_wait(barrier, n_shard - 1 + n_sec - 1)

    pair = []
    for p in range(pieces):
        loads[p][0].wait()
        c = pltpu.make_async_remote_copy(
            src_ref=away.at[:, :, :, span(p)], dst_ref=d2d.at[:, :, :, span(p)],
            send_sem=pair_sem.at[0, p], recv_sem=pair_sem.at[1, p],
            device_id=at(y, x, 1 - core), device_id_type=MESH,
        )
        c.start()
        pair.append(c)

    ones = []
    for p in range(pieces):
        loads[p][1].wait()
        pair[p].wait_recv()

        def add_pair(i, carry, p=p):
            yy, xx = i // n_x, lax.rem(i, n_x)
            total = own[yy, xx, :, span(p)].astype(jnp.float32) + d2d[yy, xx, :, span(p)].astype(jnp.float32)
            own[yy, xx, :, span(p)] = total.astype(jnp.bfloat16)
            return carry

        lax.fori_loop(0, n_y * n_x, add_pair, 0)
        group = []
        along_x = p % 2 == 0
        for j in range(1, n_x if along_x else n_y):
            if along_x:
                t = lax.rem(x + j, n_x)
                src, dst, dev = own.at[:, t, :, span(p)], r1a.at[p // 2, j - 1], at(y, t, core)
            else:
                t = lax.rem(y + j, n_y)
                src, dst, dev = own.at[t, :, :, span(p)], r1b.at[p // 2, j - 1], at(t, x, core)
            c = pltpu.make_async_remote_copy(
                src_ref=src, dst_ref=dst,
                send_sem=one_send.at[p, j - 1], recv_sem=one_recv.at[p, j - 1],
                device_id=dev, device_id_type=MESH,
            )
            c.start()
            group.append(c)
        ones.append(group)

    twos = []
    for p in range(pieces):
        for c in ones[p]:
            c.wait_recv()
        group = []
        along_x = p % 2 == 0
        for j in range(1, n_y if along_x else n_x):
            if along_x:
                t = lax.rem(y + j, n_y)
                total = own[t, x, :, span(p)].astype(jnp.float32)
                for k in range(n_x - 1):
                    total += r1a[p // 2, k, t].astype(jnp.float32)
                s1a[p // 2, j - 1] = total.astype(jnp.bfloat16)
                src, dst, dev = s1a.at[p // 2, j - 1], r2a.at[p // 2, j - 1], at(t, x, core)
            else:
                t = lax.rem(x + j, n_x)
                total = own[y, t, :, span(p)].astype(jnp.float32)
                for k in range(n_y - 1):
                    total += r1b[p // 2, k, t].astype(jnp.float32)
                s1b[p // 2, j - 1] = total.astype(jnp.bfloat16)
                src, dst, dev = s1b.at[p // 2, j - 1], r2b.at[p // 2, j - 1], at(y, t, core)
            c = pltpu.make_async_remote_copy(
                src_ref=src, dst_ref=dst,
                send_sem=two_send.at[p, j - 1], recv_sem=two_recv.at[p, j - 1],
                device_id=dev, device_id_type=MESH,
            )
            c.start()
            group.append(c)
        twos.append(group)

    def by_block(scalars):
        return jnp.concatenate([jnp.full((block_rows, LANES), s) for s in scalars], axis=0)

    layers = [layer_ref[0, b] for b in range(blocks)]
    lives = [valid_ref[0, b] for b in range(blocks)]
    row_decay = by_block([decay_ref[layer] for layer in layers])
    row_live = by_block([jnp.where(v > 0, 1.0, 0.0).astype(jnp.float32) for v in lives]) > 0.5

    for s in states:
        s.wait()

    zero = jnp.zeros((rows, LANES), jnp.float32)
    sums = (zero, zero)
    for p in range(pieces):
        for c in twos[p]:
            c.wait_recv()
        along_x = p % 2 == 0

        def update_piece(i, sums, p=p, along_x=along_x):
            usum, wsum = sums
            inner = pl.ds(pl.multiple_of(i * LANES, LANES), LANES)
            outer = pl.ds(pl.multiple_of(p * width + i * LANES, LANES), LANES)
            grad = own[y, x, :, outer].astype(jnp.float32)
            if along_x:
                for k in range(n_x - 1):
                    grad += r1a[p // 2, k, y, :, inner].astype(jnp.float32)
                for k in range(n_y - 1):
                    grad += r2a[p // 2, k, :, inner].astype(jnp.float32)
            else:
                for k in range(n_y - 1):
                    grad += r1b[p // 2, k, x, :, inner].astype(jnp.float32)
                for k in range(n_x - 1):
                    grad += r2b[p // 2, k, :, inner].astype(jnp.float32)
            weights = p_v[:, outer].astype(jnp.float32)
            old1, old2 = m1_v[:, outer], m2_v[:, outer]
            first = 0.9 * old1 + 0.1 * grad
            second = 0.99 * old2 + 0.01 * grad * grad
            update = first / bias_first / (jnp.sqrt(second / bias_second) + 1e-06) + row_decay * weights
            upd[:, outer] = update
            new1_ref[:, outer] = jnp.where(row_live, first, old1)
            new2_ref[:, outer] = jnp.where(row_live, second, old2)
            return usum + update * update, wsum + weights * weights

        sums = lax.fori_loop(0, width // LANES, update_piece, sums, unroll=2)

    n_layer = decay_ref.shape[0]
    layer_iota = lax.broadcasted_iota(jnp.int32, (n_layer, LANES), 0)
    for q in range(2):
        tile = jnp.zeros((n_layer, LANES), jnp.float32)
        for b in range(blocks):
            line = jnp.sum(sums[q][b * block_rows : (b + 1) * block_rows], axis=0, keepdims=True)
            chosen = jnp.where(lives[b] > 0, layers[b], -1)
            tile += jnp.where(layer_iota == chosen, line, 0.0)
        tiles[me, q] = tile
    sends = []
    for j in range(1, n_shard):
        t = lax.rem(me + j, n_shard)
        c = pltpu.make_async_remote_copy(
            src_ref=tiles.at[me], dst_ref=tiles.at[me],
            send_sem=t_send.at[j - 1], recv_sem=t_recv.at[j - 1],
            device_id=(sec, t), device_id_type=MESH,
        )
        c.start()
        sends.append(c)
    for c in sends:
        c.wait_recv()
    total = tiles[0]
    for j in range(1, n_shard):
        total += tiles[j]
    ztiles[sec] = total
    zsends = []
    for j in range(1, n_sec):
        c = pltpu.make_async_remote_copy(
            src_ref=ztiles.at[sec], dst_ref=ztiles.at[sec],
            send_sem=z_send.at[j - 1], recv_sem=z_recv.at[j - 1],
            device_id=(lax.rem(sec + j, n_sec), me), device_id_type=MESH,
        )
        c.start()
        zsends.append(c)
    for c in zsends:
        c.wait_recv()
    total = ztiles[0]
    for j in range(1, n_sec):
        total += ztiles[j]
    totals = jnp.sum(total, axis=-1, keepdims=True)
    ratios = jnp.sqrt(totals[1] / (totals[0] + 1.0))
    ratio_tile = jnp.broadcast_to(ratios, (n_layer, LANES))
    ratio_ref[...] = ratio_tile
    row_step = jnp.concatenate(
        [
            jnp.broadcast_to(
                0.1 * jnp.sum(
                    jnp.where((layer_iota == layers[b]) & (layer_iota >= 0) & (lives[b] > 0), ratio_tile, 0.0),
                    axis=0, keepdims=True,
                ),
                (block_rows, LANES),
            )
            for b in range(blocks)
        ],
        axis=0,
    )

    def step_piece(i, carry):
        outer = pl.ds(pl.multiple_of(i * LANES, LANES), LANES)
        weights = p_v[:, outer].astype(jnp.float32)
        stepped = weights - row_step * upd[:, outer]
        newp_ref[:, outer] = jnp.where(row_live, stepped, weights).astype(jnp.bfloat16)
        return carry

    lax.fori_loop(0, cols // LANES, step_piece, 0, unroll=4)

    for c in pair + [c for group in ones + twos for c in group] + sends + zsends:
        c.wait_send()


def shards(grad_parts, params, moment_first, moment_second, block_layer, block_valid, decay):
    n_sec, n_shard = lax.axis_size("section"), lax.axis_size("shard")
    chips = n_shard // 2
    n_y = max(d for d in range(1, math.isqrt(chips) + 1) if chips % d == 0)
    n_x = chips // n_y
    rows, cols = params.shape[1:]
    n_layer = decay.shape[0]
    pieces = PIECES
    half, width = pieces // 2, cols // pieces
    bf16, f32 = jnp.bfloat16, jnp.float32
    dma = pltpu.SemaphoreType.DMA
    most = max(n_x, n_y) - 1
    grads = grad_parts.reshape(n_y, n_x, 2, rows, cols)
    any_spec = pl.BlockSpec(memory_space=pl.ANY)
    smem = pl.BlockSpec(memory_space=pltpu.SMEM)
    vmem = pl.BlockSpec(memory_space=pltpu.VMEM)
    new_params, new_first, new_second, ratio = pl.pallas_call(
        functools.partial(kernel, n_sec, n_y, n_x, pieces),
        out_shape=(
            OUT((rows, cols), bf16),
            OUT((rows, cols), f32),
            OUT((rows, cols), f32),
            jax.ShapeDtypeStruct((n_layer, LANES), f32),
        ),
        in_specs=[any_spec] * 4 + [smem] * 3,
        out_specs=(vmem, vmem, vmem, vmem),
        scratch_shapes=[
            pltpu.VMEM((n_y, n_x, rows, cols), bf16),
            pltpu.VMEM((n_y, n_x, rows, cols), bf16),
            pltpu.VMEM((n_y, n_x, rows, cols), bf16),
            pltpu.VMEM((rows, cols), bf16),
            pltpu.VMEM((rows, cols), f32),
            pltpu.VMEM((rows, cols), f32),
            pltpu.VMEM((rows, cols), f32),
            pltpu.VMEM((half, n_x - 1, n_y, rows, width), bf16),
            pltpu.VMEM((half, n_y - 1, n_x, rows, width), bf16),
            pltpu.VMEM((half, n_y - 1, rows, width), bf16),
            pltpu.VMEM((half, n_x - 1, rows, width), bf16),
            pltpu.VMEM((half, n_y - 1, rows, width), bf16),
            pltpu.VMEM((half, n_x - 1, rows, width), bf16),
            pltpu.VMEM((n_shard, 2, n_layer, LANES), f32),
            pltpu.VMEM((n_sec, 2, n_layer, LANES), f32),
            dma((2, pieces)),
            dma((3,)),
            dma((2, pieces)),
            dma((pieces, most)),
            dma((pieces, most)),
            dma((pieces, most)),
            dma((pieces, most)),
            dma((n_shard - 1,)),
            dma((n_shard - 1,)),
            dma((n_sec - 1,)),
            dma((n_sec - 1,)),
        ],
        compiler_params=pltpu.CompilerParams(
            collective_id=0, has_side_effects=True, vmem_limit_bytes=56 * 1024 * 1024
        ),
    )(grads, params[0], moment_first[0], moment_second[0], block_layer, block_valid, decay)
    return (new_params[None], new_first[None], new_second[None], ratio[:, 0])


OUT = jax.ShapeDtypeStruct


def solution(mesh):
    placed = (
        P("section", "shard", None, None),
        P("section", "shard", None),
        P("section", "shard", None),
        P("section", "shard", None),
        P("section", "shard"),
        P("section", "shard"),
        P(),
    )
    return jax.shard_map(
        shards,
        mesh=mesh,
        in_specs=placed,
        out_specs=(
            P("section", "shard", None),
            P("section", "shard", None),
            P("section", "shard", None),
            P(),
        ),
        check_vma=False,
    )
```

time: 110 us -> 45.3 us (0.41)
  waiting for transfers between devices: 57.5 us -> 0 us
  Pallas kernels: 0 us -> 36.7 us
  blocking collectives: 31.8 us -> 0 us
  between operations: 14.1 us -> 0.64 us
  local copies, waits for them, and re-layouts: 0.34 us -> 7.69 us
  other arithmetic: 5.4 us -> 0 us
    reduce_scatter x1 -> x0, waiting for transfers between devices: 56.8 us -> none  [shards(): lax.psum_scatter(local_grad.astype(jnp.float32).astype(jnp.bfloat16), 'sh...]
    pallas_call x0 -> x1, Pallas kernels: none -> 36.7 us  [shards(): pl.pallas_call(functools.partial(kernel, n_sec, n_y, n_x, pieces), out_sh...]
    psum x2 -> x0, blocking collectives: 20.9 us -> none  [the longest x1 12.5 us: shards(): section_total = lax.psum(partial_value, 'shard')]
    all_gather x1 -> x0, blocking collectives: 10.9 us -> none  [carried_in(): gathered = lax.all_gather(part, axis)]
    unnamed x10 -> x3, local copies, waits for them, and re-layouts: 0.03 us -> 6.39 us
    reduce_sum x1 -> x0, other arithmetic: 3.8 us -> none  [shards(): jnp.sum(update * update, axis=-1)]
    slice x0 -> x1, local copies, waits for them, and re-layouts: none -> 1.3 us  [shards(): return (new_params[None], new_first[None], new_second[None], ratio[:, 0])]
  transfers between devices with their start and end apart: 1 -> 0, of which waited for: 1 -> 0; matrix products, arithmetic and copies ran while one was open for 0% -> 0% of each run, Pallas kernels for 0% -> 0%
where the time goes in v1:
time: 45.3 us; the launch traced here: 45 us
  Pallas kernels  36.7 us (81%)
  local copies, waits for them, and re-layouts  7.69 us (17%)
  between operations  0.64 us (1%)
    pallas_call x1, Pallas kernels, shards(): pl.pallas_call(functools.partial(kernel, n_sec, n_y, n_x, pieces), out_sh...  36.7 us
    unnamed x3, local copies, waits for them, and re-layouts  6.39 us
    slice x1, local copies, waits for them, and re-layouts, shards(): return (new_params[None], new_first[None], new_second[None], ratio[:, 0])  1.3 us

profile of v1, /device:TPU:0, one launch (start us, length us, event | category | flops | bytes accessed | tf_op | source)
XLA Modules:
  0.0 45.0 jit_solution(7866215579172565410)
XLA Ops:
  0.6 36.7 %shard_map.102 = (bf16[32,8192]{1,0:T(8,128)(2,1)}, f32[32,8192]{1,0:T(8,128)}, f32[32,8192]{1,0:T(8,128)}, f32[8,128]{1,0:T(8,128)}) custom-call(bf16[2,2,2,32,8192]{4,3,2,1,0:T(8,128)(2,1)} %bitcast.7, bf16[32,8192]{1,0:T(8,128)(2,1)} %bitcast.12, f32[32,8192]{1,0:T(8,128)} %bitcast.10, f32[32,8192]{1,0:T(8,128)} %bitcast.11, s32[1,4]{1,0:T(1,128)} %layer_ref.1, ...), custom_call_target="tpu_custom_call" | custom-call | tf_op jit(solution)/shard_map/pallas_call | solution.py:265
  37.4 1.3 %slice_reduce_fusion = f32[8]{0:T(128)} fusion(f32[8,128]{1,0:T(8,128)} %get-tuple-element.11), kind=kLoop, calls=%fused_computation | loop fusion | bytes 64 | tf_op jit(solution)/shard_map/slice | solution.py:307
  38.7 1.9 %copy.14 = bf16[1,32,8192]{2,1,0:T(8,128)(2,1)} copy(bf16[1,32,8192]{2,1,0:T(8,128)(2,1)} %bitcast.13) | data formatting | bytes 1048576
  40.5 2.3 %copy.15 = f32[1,32,8192]{2,1,0:T(8,128)} copy(f32[1,32,8192]{2,1,0:T(8,128)} %bitcast.9) | data formatting | bytes 2097152
  42.8 2.3 %copy.16 = f32[1,32,8192]{2,1,0:T(8,128)} copy(f32[1,32,8192]{2,1,0:T(8,128)} %bitcast.8) | data formatting | bytes 2097152

commit v2 on v1

--- a/solution.py
+++ b/solution.py
@@ -13,6 +13,7 @@
 bias_second = 1.0 - 0.99**10
 LANES = 128
 PIECES = 8
+ONE_SHOT = True
 
 
 def kernel(
@@ -56,9 +57,11 @@
     barrier = pltpu.get_barrier_semaphore()
     for j in range(1, n_shard):
         pl.semaphore_signal(barrier, inc=1, device_id=(sec, lax.rem(me + j, n_shard)), device_id_type=MESH)
-    for j in range(1, n_sec):
-        pl.semaphore_signal(barrier, inc=1, device_id=(lax.rem(sec + j, n_sec), me), device_id_type=MESH)
-    pl.semaphore_wait(barrier, n_shard - 1 + n_sec - 1)
+    for i in range(1, n_sec):
+        for j in range(n_shard if ONE_SHOT and n_shard * n_sec <= 32 else 1):
+            peer = (lax.rem(sec + i, n_sec), lax.rem(me + j, n_shard))
+            pl.semaphore_signal(barrier, inc=1, device_id=peer, device_id_type=MESH)
+    pl.semaphore_wait(barrier, n_shard - 1 + (n_sec - 1) * (n_shard if ONE_SHOT and n_shard * n_sec <= 32 else 1))
 
     pair = []
     for p in range(pieces):
@@ -177,55 +180,50 @@
         sums = lax.fori_loop(0, width // LANES, update_piece, sums, unroll=2)
 
     n_layer = decay_ref.shape[0]
-    layer_iota = lax.broadcasted_iota(jnp.int32, (n_layer, LANES), 0)
-    for q in range(2):
-        tile = jnp.zeros((n_layer, LANES), jnp.float32)
-        for b in range(blocks):
-            line = jnp.sum(sums[q][b * block_rows : (b + 1) * block_rows], axis=0, keepdims=True)
-            chosen = jnp.where(lives[b] > 0, layers[b], -1)
-            tile += jnp.where(layer_iota == chosen, line, 0.0)
-        tiles[me, q] = tile
-    sends = []
-    for j in range(1, n_shard):
-        t = lax.rem(me + j, n_shard)
-        c = pltpu.make_async_remote_copy(
-            src_ref=tiles.at[me], dst_ref=tiles.at[me],
-            send_sem=t_send.at[j - 1], recv_sem=t_recv.at[j - 1],
-            device_id=(sec, t), device_id_type=MESH,
-        )
-        c.start()
-        sends.append(c)
-    for c in sends:
-        c.wait_recv()
-    total = tiles[0]
-    for j in range(1, n_shard):
-        total += tiles[j]
-    ztiles[sec] = total
-    zsends = []
-    for j in range(1, n_sec):
-        c = pltpu.make_async_remote_copy(
-            src_ref=ztiles.at[sec], dst_ref=ztiles.at[sec],
-            send_sem=z_send.at[j - 1], recv_sem=z_recv.at[j - 1],
-            device_id=(lax.rem(sec + j, n_sec), me), device_id_type=MESH,
-        )
-        c.start()
-        zsends.append(c)
-    for c in zsends:
-        c.wait_recv()
-    total = ztiles[0]
-    for j in range(1, n_sec):
-        total += ztiles[j]
-    totals = jnp.sum(total, axis=-1, keepdims=True)
-    ratios = jnp.sqrt(totals[1] / (totals[0] + 1.0))
-    ratio_tile = jnp.broadcast_to(ratios, (n_layer, LANES))
-    ratio_ref[...] = ratio_tile
+    lane = lax.broadcasted_iota(jnp.int32, (1, LANES), 1)
+    line = jnp.zeros((1, LANES), jnp.float32)
+    for b in range(blocks):
+        chosen = jnp.where(lives[b] > 0, layers[b], -LANES)
+        for q, values in enumerate((sums[1], sums[0])):
+            part = jnp.sum(values[b * block_rows : (b + 1) * block_rows], axis=0, keepdims=True)
+            line += jnp.where(lane == chosen + q * n_layer, jnp.sum(part, axis=1, keepdims=True), 0.0)
+
+    def all_sum(line, slots, send_sem, recv_sem, index, peers):
+        slots[index] = line
+        copies = []
+        for j, peer in enumerate(peers):
+            c = pltpu.make_async_remote_copy(
+                src_ref=slots.at[index], dst_ref=slots.at[index],
+                send_sem=send_sem.at[j], recv_sem=recv_sem.at[j],
+                device_id=peer, device_id_type=MESH,
+            )
+            c.start()
+            copies.append(c)
+        for c in copies:
+            c.wait_recv()
+        total = slots[0]
+        for j in range(1, len(peers) + 1):
+            total += slots[j]
+        return total, copies
+
+    shard_peers = [(sec, lax.rem(me + j, n_shard)) for j in range(1, n_shard)]
+    sec_peers = [(lax.rem(sec + j, n_sec), me) for j in range(1, n_sec)]
+    if ONE_SHOT and n_shard * n_sec <= 32:
+        every = [
+            (lax.rem(sec + i, n_sec), lax.rem(me + j, n_shard))
+            for i in range(n_sec) for j in range(n_shard) if i or j
+        ]
+        line, sends = all_sum(line, tiles, t_send, t_recv, sec * n_shard + me, every[::-1])
+    else:
+        line, sends = all_sum(line, tiles, t_send, t_recv, me, shard_peers)
+        line, zsends = all_sum(line, ztiles, z_send, z_recv, sec, sec_peers)
+        sends += zsends
+    ratios = jnp.sqrt(line / (pltpu.roll(line, LANES - n_layer, 1) + 1.0))
+    ratio_ref[...] = ratios
     row_step = jnp.concatenate(
         [
             jnp.broadcast_to(
-                0.1 * jnp.sum(
-                    jnp.where((layer_iota == layers[b]) & (layer_iota >= 0) & (lives[b] > 0), ratio_tile, 0.0),
-                    axis=0, keepdims=True,
-                ),
+                0.1 * jnp.sum(jnp.where(lane == layers[b], ratios, 0.0), axis=1, keepdims=True),
                 (block_rows, LANES),
             )
             for b in range(blocks)
@@ -242,8 +240,20 @@
 
     lax.fori_loop(0, cols // LANES, step_piece, 0, unroll=4)
 
-    for c in pair + [c for group in ones + twos for c in group] + sends + zsends:
+    for c in pair + [c for group in ones + twos for c in group] + sends:
         c.wait_send()
+
+
+def finish(newp_v, new1_v, new2_v, ratio_v, newp_hbm, new1_hbm, new2_hbm, ratio_ref, sem):
+    copies = [
+        pltpu.make_async_copy(src, dst, sem.at[i])
+        for i, (src, dst) in enumerate(((new1_v, new1_hbm), (new2_v, new2_hbm), (newp_v, newp_hbm)))
+    ]
+    for c in copies:
+        c.start()
+    ratio_ref[...] = ratio_v[0, : ratio_ref.shape[0]]
+    for c in copies:
+        c.wait()
 
 
 def shards(grad_parts, params, moment_first, moment_second, block_layer, block_valid, decay):
@@ -257,18 +267,19 @@
     half, width = pieces // 2, cols // pieces
     bf16, f32 = jnp.bfloat16, jnp.float32
     dma = pltpu.SemaphoreType.DMA
+    n_lines = n_shard * n_sec if ONE_SHOT and n_shard * n_sec <= 32 else n_shard
     most = max(n_x, n_y) - 1
     grads = grad_parts.reshape(n_y, n_x, 2, rows, cols)
-    any_spec = pl.BlockSpec(memory_space=pl.ANY)
+    any_spec = pl.BlockSpec(memory_space=pltpu.HBM)
     smem = pl.BlockSpec(memory_space=pltpu.SMEM)
     vmem = pl.BlockSpec(memory_space=pltpu.VMEM)
     new_params, new_first, new_second, ratio = pl.pallas_call(
         functools.partial(kernel, n_sec, n_y, n_x, pieces),
         out_shape=(
-            OUT((rows, cols), bf16),
-            OUT((rows, cols), f32),
-            OUT((rows, cols), f32),
-            jax.ShapeDtypeStruct((n_layer, LANES), f32),
+            pltpu.VMEM((rows, cols), bf16),
+            pltpu.VMEM((rows, cols), f32),
+            pltpu.VMEM((rows, cols), f32),
+            pltpu.VMEM((1, LANES), f32),
         ),
         in_specs=[any_spec] * 4 + [smem] * 3,
         out_specs=(vmem, vmem, vmem, vmem),
@@ -286,8 +297,8 @@
             pltpu.VMEM((half, n_x - 1, rows, width), bf16),
             pltpu.VMEM((half, n_y - 1, rows, width), bf16),
             pltpu.VMEM((half, n_x - 1, rows, width), bf16),
-            pltpu.VMEM((n_shard, 2, n_layer, LANES), f32),
-            pltpu.VMEM((n_sec, 2, n_layer, LANES), f32),
+            pltpu.VMEM((n_lines, 1, LANES), f32),
+            pltpu.VMEM((n_sec, 1, LANES), f32),
             dma((2, pieces)),
             dma((3,)),
             dma((2, pieces)),
@@ -295,19 +306,29 @@
             dma((pieces, most)),
             dma((pieces, most)),
             dma((pieces, most)),
-            dma((n_shard - 1,)),
-            dma((n_shard - 1,)),
+            dma((n_lines - 1,)),
+            dma((n_lines - 1,)),
             dma((n_sec - 1,)),
             dma((n_sec - 1,)),
         ],
         compiler_params=pltpu.CompilerParams(
-            collective_id=0, has_side_effects=True, vmem_limit_bytes=56 * 1024 * 1024
+            collective_id=0, has_side_effects=True, vmem_limit_bytes=60 * 1024 * 1024
         ),
     )(grads, params[0], moment_first[0], moment_second[0], block_layer, block_valid, decay)
-    return (new_params[None], new_first[None], new_second[None], ratio[:, 0])
-
-
-OUT = jax.ShapeDtypeStruct
+    out = pl.pallas_call(
+        finish,
+        out_shape=(
+            jax.ShapeDtypeStruct((rows, cols), bf16),
+            jax.ShapeDtypeStruct((rows, cols), f32),
+            jax.ShapeDtypeStruct((rows, cols), f32),
+            jax.ShapeDtypeStruct((n_layer,), f32),
+        ),
+        in_specs=[vmem] * 4,
+        out_specs=(any_spec, any_spec, any_spec, vmem),
+        scratch_shapes=[dma((3,))],
+        compiler_params=pltpu.CompilerParams(vmem_limit_bytes=8 * 1024 * 1024),
+    )(new_params, new_first, new_second, ratio)
+    return (out[0][None], out[1][None], out[2][None], out[3])
 
 
 def solution(mesh):

time: 45.3 us -> 36.5 us (0.81)
  local copies, waits for them, and re-layouts: 7.69 us -> 0 us
  Pallas kernels: 36.7 us -> 35.7 us
    unnamed x3 -> x0, local copies, waits for them, and re-layouts: 6.39 us -> none
    pallas_call x1, Pallas kernels: 36.7 us -> 33.7 us  [shards(): pl.pallas_call(functools.partial(kernel, n_sec, n_y, n_x, pieces), out_sh...]
    pallas_call x0 -> x1, Pallas kernels: none -> 2.02 us  [shards(): pl.pallas_call(finish, out_shape=(jax.ShapeDtypeStruct((rows, cols), bf16...]
    slice x1 -> x0, local copies, waits for them, and re-layouts: 1.3 us -> none  [shards(): return (new_params[None], new_first[None], new_second[None], ratio[:, 0])]
where the time goes in v2:
time: 36.5 us; the launch traced here: 36.4 us
  Pallas kernels  35.7 us (98%)
  between operations  0.64 us (2%)
    pallas_call x1, Pallas kernels, shards(): pl.pallas_call(functools.partial(kernel, n_sec, n_y, n_x, pieces), out_sh...  33.7 us
    pallas_call x1, Pallas kernels, shards(): pl.pallas_call(finish, out_shape=(jax.ShapeDtypeStruct((rows, cols), bf16...  2.02 us

profile of v2, /device:TPU:0, one launch (start us, length us, event | category | flops | bytes accessed | tf_op | source)
XLA Modules:
  0.0 36.4 jit_solution(8903605736058109555)
XLA Ops:
  0.6 33.7 %shard_map.102 = (bf16[32,8192]{1,0:T(8,128)(2,1)S(1)}, f32[32,8192]{1,0:T(8,128)S(1)}, f32[32,8192]{1,0:T(8,128)S(1)}, f32[1,128]{1,0:T(1,128)S(1)}) custom-call(bf16[2,2,2,32,8192]{4,3,2,1,0:T(8,128)(2,1)} %bitcast.7, bf16[32,8192]{1,0:T(8,128)(2,1)} %bitcast.10, f32[32,8192]{1,0:T(8,128)} %bitcast.8, f32[32,8192]{1,0:T(8,128)} %bitcast.9, ...), custom_call_target="tpu_custom_call" | custom-call | tf_op jit(solution)/shard_map/pallas_call | solution.py:276
  34.3 2.0 %shard_map.103 = (bf16[32,8192]{1,0:T(8,128)(2,1)}, f32[32,8192]{1,0:T(8,128)}, f32[32,8192]{1,0:T(8,128)}, f32[8]{0:T(128)}) custom-call(bf16[32,8192]{1,0:T(8,128)(2,1)S(1)} %get-tuple-element.12.newp_v, f32[32,8192]{1,0:T(8,128)S(1)} %get-tuple-element.13.new1_v, f32[32,8192]{1,0:T(8,128)S(1)} %get-tuple-element.14.new2_v, ...), custom_call_target="tpu_custom_call" | custom-call | tf_op jit(solution)/shard_map/pallas_call | solution.py:318

commit v3 on v2

--- a/solution.py
+++ b/solution.py
@@ -14,15 +14,16 @@
 LANES = 128
 PIECES = 8
 ONE_SHOT = True
+PARTS = 2
 
 
 def kernel(
     n_sec, n_y, n_x, pieces,
     g_hbm, p_hbm, m1_hbm, m2_hbm, layer_ref, valid_ref, decay_ref,
-    newp_ref, new1_ref, new2_ref, ratio_ref,
-    own, away, d2d, p_v, m1_v, m2_v, upd, r1a, r1b, s1a, s1b, r2a, r2b, tiles, ztiles,
+    p_v, upd, new1_ref, new2_ref, step_ref, ratio_ref,
+    own, away, d2d, m1_v, m2_v, r1a, r1b, s1a, s1b, r2a, r2b, tiles, ztiles,
     load_sem, state_sem, pair_sem, one_send, one_recv, two_send, two_recv,
-    t_send, t_recv, z_send, z_recv,
+    t_send, t_recv, z_send, z_recv, told,
 ):
     rows, cols = p_v.shape
     width = cols // pieces
@@ -55,13 +56,46 @@
         s.start()
 
     barrier = pltpu.get_barrier_semaphore()
-    for j in range(1, n_shard):
-        pl.semaphore_signal(barrier, inc=1, device_id=(sec, lax.rem(me + j, n_shard)), device_id_type=MESH)
-    for i in range(1, n_sec):
-        for j in range(n_shard if ONE_SHOT and n_shard * n_sec <= 32 else 1):
-            peer = (lax.rem(sec + i, n_sec), lax.rem(me + j, n_shard))
-            pl.semaphore_signal(barrier, inc=1, device_id=peer, device_id_type=MESH)
-    pl.semaphore_wait(barrier, n_shard - 1 + (n_sec - 1) * (n_shard if ONE_SHOT and n_shard * n_sec <= 32 else 1))
+    near = [at(y, x, 1 - core)]
+    near += [at(y, lax.rem(x + j, n_x), core) for j in range(1, n_x)]
+    near += [at(lax.rem(y + j, n_y), x, core) for j in range(1, n_y)]
+    for peer in near:
+        pl.semaphore_signal(barrier, inc=1, device_id=peer, device_id_type=MESH)
+    last_sec = n_sec - 1
+    up = (jnp.minimum(sec + 1, last_sec), me)
+    down = (jnp.maximum(sec - 1, 0), me)
+
+    @pl.when(sec < last_sec)
+    def _():
+        pl.semaphore_signal(barrier, inc=1, device_id=up, device_id_type=MESH)
+
+    @pl.when(sec > 0)
+    def _():
+        pl.semaphore_signal(barrier, inc=1, device_id=down, device_id_type=MESH)
+
+    ends = jnp.where(sec < last_sec, 1, 0) + jnp.where(sec > 0, 1, 0)
+    pl.semaphore_wait(barrier, len(near) + ends)
+
+    def relay(d):
+        if d > 1:
+
+            @pl.when(sec >= d - 1)
+            def _():
+                pl.semaphore_wait(told.at[0, d - 2], 1)
+
+            @pl.when(sec <= n_sec - d)
+            def _():
+                pl.semaphore_wait(told.at[1, d - 2], 1)
+
+        if d < n_sec:
+
+            @pl.when((sec >= d - 1) & (sec < last_sec))
+            def _():
+                pl.semaphore_signal(told.at[0, d - 1], inc=1, device_id=up, device_id_type=MESH)
+
+            @pl.when((sec <= n_sec - d) & (sec > 0))
+            def _():
+                pl.semaphore_signal(told.at[1, d - 1], inc=1, device_id=down, device_id_type=MESH)
 
     pair = []
     for p in range(pieces):
@@ -171,13 +205,18 @@
             old1, old2 = m1_v[:, outer], m2_v[:, outer]
             first = 0.9 * old1 + 0.1 * grad
             second = 0.99 * old2 + 0.01 * grad * grad
-            update = first / bias_first / (jnp.sqrt(second / bias_second) + 1e-06) + row_decay * weights
+            update = first * (1.0 / bias_first) / (jnp.sqrt(second * (1.0 / bias_second)) + 1e-06) + row_decay * weights
             upd[:, outer] = update
             new1_ref[:, outer] = jnp.where(row_live, first, old1)
             new2_ref[:, outer] = jnp.where(row_live, second, old2)
             return usum + update * update, wsum + weights * weights
 
         sums = lax.fori_loop(0, width // LANES, update_piece, sums, unroll=2)
+        if p < n_sec:
+            relay(p + 1)
+
+    for d in range(pieces, n_sec):
+        relay(d + 1)
 
     n_layer = decay_ref.shape[0]
     lane = lax.broadcasted_iota(jnp.int32, (1, LANES), 1)
@@ -220,10 +259,12 @@
         sends += zsends
     ratios = jnp.sqrt(line / (pltpu.roll(line, LANES - n_layer, 1) + 1.0))
     ratio_ref[...] = ratios
-    row_step = jnp.concatenate(
+    step_ref[...] = jnp.concatenate(
         [
             jnp.broadcast_to(
-                0.1 * jnp.sum(jnp.where(lane == layers[b], ratios, 0.0), axis=1, keepdims=True),
+                0.1 * jnp.sum(
+                    jnp.where((lane == layers[b]) & (lives[b] > 0), ratios, 0.0), axis=1, keepdims=True
+                ),
                 (block_rows, LANES),
             )
             for b in range(blocks)
@@ -231,27 +272,35 @@
         axis=0,
     )
 
-    def step_piece(i, carry):
-        outer = pl.ds(pl.multiple_of(i * LANES, LANES), LANES)
-        weights = p_v[:, outer].astype(jnp.float32)
-        stepped = weights - row_step * upd[:, outer]
-        newp_ref[:, outer] = jnp.where(row_live, stepped, weights).astype(jnp.bfloat16)
-        return carry
-
-    lax.fori_loop(0, cols // LANES, step_piece, 0, unroll=4)
-
     for c in pair + [c for group in ones + twos for c in group] + sends:
         c.wait_send()
 
 
-def finish(newp_v, new1_v, new2_v, ratio_v, newp_hbm, new1_hbm, new2_hbm, ratio_ref, sem):
-    copies = [
-        pltpu.make_async_copy(src, dst, sem.at[i])
-        for i, (src, dst) in enumerate(((new1_v, new1_hbm), (new2_v, new2_hbm), (newp_v, newp_hbm)))
-    ]
-    for c in copies:
+def finish(parts, p_v, upd, new1_v, new2_v, step_v, ratio_v, newp_hbm, new1_hbm, new2_hbm, ratio_ref, newp_v, sem):
+    cols = p_v.shape[1]
+    width = cols // parts
+    copies = []
+    for k in range(parts):
+        span = pl.ds(k * width, width)
+        for i, (src, dst) in enumerate(((new1_v, new1_hbm), (new2_v, new2_hbm))):
+            c = pltpu.make_async_copy(src.at[:, span], dst.at[:, span], sem.at[i, k])
+            c.start()
+            copies.append(c)
+    ratio_ref[...] = ratio_v[0, : ratio_ref.shape[0]]
+    row_step = step_v[...]
+
+    for k in range(parts):
+        def step_piece(i, carry, k=k):
+            outer = pl.ds(pl.multiple_of(k * width + i * LANES, LANES), LANES)
+            stepped = p_v[:, outer].astype(jnp.float32) - row_step * upd[:, outer]
+            newp_v[:, outer] = stepped.astype(jnp.bfloat16)
+            return carry
+
+        lax.fori_loop(0, width // LANES, step_piece, 0, unroll=4)
+        span = pl.ds(k * width, width)
+        c = pltpu.make_async_copy(newp_v.at[:, span], newp_hbm.at[:, span], sem.at[2, k])
         c.start()
-    ratio_ref[...] = ratio_v[0, : ratio_ref.shape[0]]
+        copies.append(c)
     for c in copies:
         c.wait()
 
@@ -273,22 +322,22 @@
     any_spec = pl.BlockSpec(memory_space=pltpu.HBM)
     smem = pl.BlockSpec(memory_space=pltpu.SMEM)
     vmem = pl.BlockSpec(memory_space=pltpu.VMEM)
-    new_params, new_first, new_second, ratio = pl.pallas_call(
+    held = pl.pallas_call(
         functools.partial(kernel, n_sec, n_y, n_x, pieces),
         out_shape=(
             pltpu.VMEM((rows, cols), bf16),
             pltpu.VMEM((rows, cols), f32),
             pltpu.VMEM((rows, cols), f32),
+            pltpu.VMEM((rows, cols), f32),
+            pltpu.VMEM((rows, LANES), f32),
             pltpu.VMEM((1, LANES), f32),
         ),
         in_specs=[any_spec] * 4 + [smem] * 3,
-        out_specs=(vmem, vmem, vmem, vmem),
+        out_specs=(vmem,) * 6,
         scratch_shapes=[
             pltpu.VMEM((n_y, n_x, rows, cols), bf16),
             pltpu.VMEM((n_y, n_x, rows, cols), bf16),
             pltpu.VMEM((n_y, n_x, rows, cols), bf16),
-            pltpu.VMEM((rows, cols), bf16),
-            pltpu.VMEM((rows, cols), f32),
             pltpu.VMEM((rows, cols), f32),
             pltpu.VMEM((rows, cols), f32),
             pltpu.VMEM((half, n_x - 1, n_y, rows, width), bf16),
@@ -310,24 +359,25 @@
             dma((n_lines - 1,)),
             dma((n_sec - 1,)),
             dma((n_sec - 1,)),
+            pltpu.SemaphoreType.REGULAR((2, n_sec - 1)),
         ],
         compiler_params=pltpu.CompilerParams(
-            collective_id=0, has_side_effects=True, vmem_limit_bytes=60 * 1024 * 1024
+            collective_id=0, has_side_effects=True, vmem_limit_bytes=56 * 1024 * 1024
         ),
     )(grads, params[0], moment_first[0], moment_second[0], block_layer, block_valid, decay)
     out = pl.pallas_call(
-        finish,
+        functools.partial(finish, PARTS),
         out_shape=(
             jax.ShapeDtypeStruct((rows, cols), bf16),
             jax.ShapeDtypeStruct((rows, cols), f32),
             jax.ShapeDtypeStruct((rows, cols), f32),
             jax.ShapeDtypeStruct((n_layer,), f32),
         ),
-        in_specs=[vmem] * 4,
+        in_specs=[vmem] * 6,
         out_specs=(any_spec, any_spec, any_spec, vmem),
-        scratch_shapes=[dma((3,))],
+        scratch_shapes=[pltpu.VMEM((rows, cols), bf16), dma((3, PARTS))],
         compiler_params=pltpu.CompilerParams(vmem_limit_bytes=8 * 1024 * 1024),
-    )(new_params, new_first, new_second, ratio)
+    )(*held)
     return (out[0][None], out[1][None], out[2][None], out[3])
 
 

time: 36.5 us -> 35.6 us (0.975)
  Pallas kernels: 35.7 us -> 34.8 us
    pallas_call x1, Pallas kernels: 33.7 us -> 32.7 us  [shards(): pl.pallas_call(functools.partial(kernel, n_sec, n_y, n_x, pieces), out_sh...]
where the time goes in v3:
time: 35.6 us; the launch traced here: 35.4 us
  Pallas kernels  34.8 us (98%)
  between operations  0.64 us (2%)
    pallas_call x1, Pallas kernels, shards(): pl.pallas_call(functools.partial(kernel, n_sec, n_y, n_x, pieces), out_sh...  32.7 us
    pallas_call x1, Pallas kernels, shards(): pl.pallas_call(functools.partial(finish, PARTS), out_shape=(jax.ShapeDtyp...  2.04 us

profile of v3, /device:TPU:0, one launch (start us, length us, event | category | flops | bytes accessed | tf_op | source)
XLA Modules:
  0.0 35.4 jit_solution(13870660191322214998)
XLA Ops:
  0.6 32.7 %shard_map.102 = (bf16[32,8192]{1,0:T(8,128)(2,1)S(1)}, f32[32,8192]{1,0:T(8,128)S(1)}, f32[32,8192]{1,0:T(8,128)S(1)}, f32[32,8192]{1,0:T(8,128)S(1)}, f32[32,128]{1,0:T(8,128)S(1)}, /*index=5*/f32[1,128]{1,0:T(1,128)S(1)}) custom-call(bf16[2,2,2,32,8192]{4,3,2,1,0:T(8,128)(2,1)} %bitcast.7, bf16[32,8192]{1,0:T(8,128)(2,1)} %bitcast.10, ...), custom_call_target="tpu_custom_call" | custom-call | tf_op jit(solution)/shard_map/pallas_call | solution.py:325
  33.4 2.0 %shard_map.103 = (bf16[32,8192]{1,0:T(8,128)(2,1)}, f32[32,8192]{1,0:T(8,128)}, f32[32,8192]{1,0:T(8,128)}, f32[8]{0:T(128)}) custom-call(bf16[32,8192]{1,0:T(8,128)(2,1)S(1)} %get-tuple-element.14.p_v, f32[32,8192]{1,0:T(8,128)S(1)} %get-tuple-element.15.upd, f32[32,8192]{1,0:T(8,128)S(1)} %get-tuple-element.16.new1_v, ...), custom_call_target="tpu_custom_call" | custom-call | tf_op jit(solution)/shard_map/pallas_call | solution.py:368

commit v4 on v3

--- a/solution.py
+++ b/solution.py
@@ -23,10 +23,11 @@
     p_v, upd, new1_ref, new2_ref, step_ref, ratio_ref,
     own, away, d2d, m1_v, m2_v, r1a, r1b, s1a, s1b, r2a, r2b, tiles, ztiles,
     load_sem, state_sem, pair_sem, one_send, one_recv, two_send, two_recv,
-    t_send, t_recv, z_send, z_recv, told,
+    t_send, t_recv, z_send, z_recv, told, xa, xb, raw_send, raw_recv,
 ):
     rows, cols = p_v.shape
     width = cols // pieces
+    raw = xa.shape[-1]
     n_shard = 2 * n_y * n_x
     sec, me = lax.axis_index("section"), lax.axis_index("shard")
     core = lax.rem(me, 2)
@@ -57,8 +58,9 @@
 
     barrier = pltpu.get_barrier_semaphore()
     near = [at(y, x, 1 - core)]
-    near += [at(y, lax.rem(x + j, n_x), core) for j in range(1, n_x)]
-    near += [at(lax.rem(y + j, n_y), x, core) for j in range(1, n_y)]
+    for cc in (core, 1 - core):
+        near += [at(y, lax.rem(x + j, n_x), cc) for j in range(1, n_x)]
+        near += [at(lax.rem(y + j, n_y), x, cc) for j in range(1, n_y)]
     for peer in near:
         pl.semaphore_signal(barrier, inc=1, device_id=peer, device_id_type=MESH)
     last_sec = n_sec - 1
@@ -96,6 +98,31 @@
             @pl.when((sec <= n_sec - d) & (sec > 0))
             def _():
                 pl.semaphore_signal(told.at[1, d - 1], inc=1, device_id=down, device_id_type=MESH)
+
+    def raw_span(p):
+        return pl.ds(p * width, raw)
+
+    def send_raw(p):
+        loads[p][1].wait()
+        group = []
+        for j in range(1, n_y if p else n_x):
+            for which, (buffer, cc) in enumerate(((own, core), (away, 1 - core))):
+                if p == 0:
+                    t = lax.rem(x + j, n_x)
+                    src, dev = buffer.at[:, t, :, raw_span(p)], at(y, t, cc)
+                else:
+                    t = lax.rem(y + j, n_y)
+                    src, dev = buffer.at[t, :, :, raw_span(p)], at(t, x, cc)
+                first_dst, other_dst = (r1b, xb) if p else (r1a, xa)
+                c = pltpu.make_async_remote_copy(
+                    src_ref=src,
+                    dst_ref=other_dst.at[j - 1] if which else first_dst.at[0, j - 1, :, :, pl.ds(0, raw)],
+                    send_sem=raw_send.at[p, which, j - 1], recv_sem=raw_recv.at[p, which, j - 1],
+                    device_id=dev, device_id_type=MESH,
+                )
+                c.start()
+                group.append(c)
+        return group
 
     pair = []
     for p in range(pieces):
@@ -107,28 +134,38 @@
         )
         c.start()
         pair.append(c)
+        if p == 1:
+            raws = [send_raw(0), send_raw(1)]
 
     ones = []
     for p in range(pieces):
-        loads[p][1].wait()
+        if p > 1:
+            loads[p][1].wait()
         pair[p].wait_recv()
-
-        def add_pair(i, carry, p=p):
-            yy, xx = i // n_x, lax.rem(i, n_x)
-            total = own[yy, xx, :, span(p)].astype(jnp.float32) + d2d[yy, xx, :, span(p)].astype(jnp.float32)
-            own[yy, xx, :, span(p)] = total.astype(jnp.bfloat16)
+        along_x = p % 2 == 0
+        skip = raw if p < 2 else 0
+        rest = pl.ds(p * width + skip, width - skip)
+
+        def add_pair(yy, xx, cut):
+            total = own[yy, xx, :, cut].astype(jnp.float32) + d2d[yy, xx, :, cut].astype(jnp.float32)
+            own[yy, xx, :, cut] = total.astype(jnp.bfloat16)
+
+        def add_all(i, carry, rest=rest):
+            add_pair(i // n_x, lax.rem(i, n_x), rest)
             return carry
 
-        lax.fori_loop(0, n_y * n_x, add_pair, 0)
+        lax.fori_loop(0, n_y * n_x, add_all, 0)
         group = []
-        along_x = p % 2 == 0
         for j in range(1, n_x if along_x else n_y):
+            landing = pl.ds(skip, width - skip)
             if along_x:
                 t = lax.rem(x + j, n_x)
-                src, dst, dev = own.at[:, t, :, span(p)], r1a.at[p // 2, j - 1], at(y, t, core)
+                src, dev = own.at[:, t, :, rest], at(y, t, core)
+                dst = r1a.at[p // 2, j - 1, :, :, landing]
             else:
                 t = lax.rem(y + j, n_y)
-                src, dst, dev = own.at[t, :, :, span(p)], r1b.at[p // 2, j - 1], at(t, x, core)
+                src, dev = own.at[t, :, :, rest], at(t, x, core)
+                dst = r1b.at[p // 2, j - 1, :, :, landing]
             c = pltpu.make_async_remote_copy(
                 src_ref=src, dst_ref=dst,
                 send_sem=one_send.at[p, j - 1], recv_sem=one_recv.at[p, j - 1],
@@ -137,11 +174,21 @@
             c.start()
             group.append(c)
         ones.append(group)
+        if p < 2:
+            for i in range(n_y if along_x else n_x):
+                add_pair(i if along_x else y, x if along_x else i, raw_span(p))
 
     twos = []
     for p in range(pieces):
         for c in ones[p]:
             c.wait_recv()
+        if p < 2:
+            for c in raws[p]:
+                c.wait_recv()
+            for k in range(n_y - 1 if p else n_x - 1):
+                landed, other = (r1b, xb) if p else (r1a, xa)
+                total = landed[0, k, :, :, :raw].astype(jnp.float32) + other[k].astype(jnp.float32)
+                landed[0, k, :, :, :raw] = total.astype(jnp.bfloat16)
         group = []
         along_x = p % 2 == 0
         for j in range(1, n_y if along_x else n_x):
@@ -252,7 +299,7 @@
             (lax.rem(sec + i, n_sec), lax.rem(me + j, n_shard))
             for i in range(n_sec) for j in range(n_shard) if i or j
         ]
-        line, sends = all_sum(line, tiles, t_send, t_recv, sec * n_shard + me, every[::-1])
+        line, sends = all_sum(line, tiles, t_send, t_recv, sec * n_shard + me, every)
     else:
         line, sends = all_sum(line, tiles, t_send, t_recv, me, shard_peers)
         line, zsends = all_sum(line, ztiles, z_send, z_recv, sec, sec_peers)
@@ -272,7 +319,7 @@
         axis=0,
     )
 
-    for c in pair + [c for group in ones + twos for c in group] + sends:
+    for c in pair + [c for group in raws + ones + twos for c in group] + sends:
         c.wait_send()
 
 
@@ -314,6 +361,7 @@
     n_layer = decay.shape[0]
     pieces = PIECES
     half, width = pieces // 2, cols // pieces
+    raw = width * 3 // 8 // LANES * LANES
     bf16, f32 = jnp.bfloat16, jnp.float32
     dma = pltpu.SemaphoreType.DMA
     n_lines = n_shard * n_sec if ONE_SHOT and n_shard * n_sec <= 32 else n_shard
@@ -360,6 +408,10 @@
             dma((n_sec - 1,)),
             dma((n_sec - 1,)),
             pltpu.SemaphoreType.REGULAR((2, n_sec - 1)),
+            pltpu.VMEM((n_x - 1, n_y, rows, raw), bf16),
+            pltpu.VMEM((n_y - 1, n_x, rows, raw), bf16),
+            dma((2, 2, most)),
+            dma((2, 2, most)),
         ],
         compiler_params=pltpu.CompilerParams(
             collective_id=0, has_side_effects=True, vmem_limit_bytes=56 * 1024 * 1024

time: 35.6 us -> 35.3 us (level)
  no operation moved by 1% of the time
where the time goes in v4:
time: 35.3 us; the launch traced here: 35.1 us
  Pallas kernels  34.5 us (98%)
  between operations  0.64 us (2%)
    pallas_call x1, Pallas kernels, shards(): pl.pallas_call(functools.partial(kernel, n_sec, n_y, n_x, pieces), out_sh...  32.4 us
    pallas_call x1, Pallas kernels, shards(): pl.pallas_call(functools.partial(finish, PARTS), out_shape=(jax.ShapeDtyp...  2.04 us

profile of v4, /device:TPU:0, one launch (start us, length us, event | category | flops | bytes accessed | tf_op | source)
XLA Modules:
  0.0 35.1 jit_solution(1297390592544228984)
XLA Ops:
  0.6 32.4 %shard_map.102 = (bf16[32,8192]{1,0:T(8,128)(2,1)S(1)}, f32[32,8192]{1,0:T(8,128)S(1)}, f32[32,8192]{1,0:T(8,128)S(1)}, f32[32,8192]{1,0:T(8,128)S(1)}, f32[32,128]{1,0:T(8,128)S(1)}, /*index=5*/f32[1,128]{1,0:T(1,128)S(1)}) custom-call(bf16[2,2,2,32,8192]{4,3,2,1,0:T(8,128)(2,1)} %bitcast.7, bf16[32,8192]{1,0:T(8,128)(2,1)} %bitcast.10, ...), custom_call_target="tpu_custom_call" | custom-call | tf_op jit(solution)/shard_map/pallas_call | solution.py:373
  33.1 2.0 %shard_map.103 = (bf16[32,8192]{1,0:T(8,128)(2,1)}, f32[32,8192]{1,0:T(8,128)}, f32[32,8192]{1,0:T(8,128)}, f32[8]{0:T(128)}) custom-call(bf16[32,8192]{1,0:T(8,128)(2,1)S(1)} %get-tuple-element.14.p_v, f32[32,8192]{1,0:T(8,128)S(1)} %get-tuple-element.15.upd, f32[32,8192]{1,0:T(8,128)S(1)} %get-tuple-element.16.new1_v, ...), custom_call_target="tpu_custom_call" | custom-call | tf_op jit(solution)/shard_map/pallas_call | solution.py:420

commit v5 on v4

--- a/solution.py
+++ b/solution.py
@@ -267,12 +267,13 @@
 
     n_layer = decay_ref.shape[0]
     lane = lax.broadcasted_iota(jnp.int32, (1, LANES), 1)
-    line = jnp.zeros((1, LANES), jnp.float32)
+    lines = []
     for b in range(blocks):
         chosen = jnp.where(lives[b] > 0, layers[b], -LANES)
         for q, values in enumerate((sums[1], sums[0])):
-            part = jnp.sum(values[b * block_rows : (b + 1) * block_rows], axis=0, keepdims=True)
-            line += jnp.where(lane == chosen + q * n_layer, jnp.sum(part, axis=1, keepdims=True), 0.0)
+            block = values[b * block_rows : (b + 1) * block_rows]
+            lines.append(jnp.where(lane == chosen + q * n_layer, jnp.sum(block, axis=1, keepdims=True), 0.0))
+    line = jnp.sum(sum(lines[1:], lines[0]), axis=0, keepdims=True)
 
     def all_sum(line, slots, send_sem, recv_sem, index, peers):
         slots[index] = line

time: 35.3 us -> 35.3 us (level)
  no operation moved by 1% of the time
where the time goes in v5:
time: 35.3 us; the launch traced here: 35.1 us
  Pallas kernels  34.5 us (98%)
  between operations  0.64 us (2%)
    pallas_call x1, Pallas kernels, shards(): pl.pallas_call(functools.partial(kernel, n_sec, n_y, n_x, pieces), out_sh...  32.4 us
    pallas_call x1, Pallas kernels, shards(): pl.pallas_call(functools.partial(finish, PARTS), out_shape=(jax.ShapeDtyp...  2.04 us

profile of v5, /device:TPU:0, one launch (start us, length us, event | category | flops | bytes accessed | tf_op | source)
XLA Modules:
  0.0 35.1 jit_solution(13872892829003689602)
XLA Ops:
  0.6 32.4 %shard_map.102 = (bf16[32,8192]{1,0:T(8,128)(2,1)S(1)}, f32[32,8192]{1,0:T(8,128)S(1)}, f32[32,8192]{1,0:T(8,128)S(1)}, f32[32,8192]{1,0:T(8,128)S(1)}, f32[32,128]{1,0:T(8,128)S(1)}, /*index=5*/f32[1,128]{1,0:T(1,128)S(1)}) custom-call(bf16[2,2,2,32,8192]{4,3,2,1,0:T(8,128)(2,1)} %bitcast.7, bf16[32,8192]{1,0:T(8,128)(2,1)} %bitcast.10, ...), custom_call_target="tpu_custom_call" | custom-call | tf_op jit(solution)/shard_map/pallas_call | solution.py:374
  33.1 2.0 %shard_map.103 = (bf16[32,8192]{1,0:T(8,128)(2,1)}, f32[32,8192]{1,0:T(8,128)}, f32[32,8192]{1,0:T(8,128)}, f32[8]{0:T(128)}) custom-call(bf16[32,8192]{1,0:T(8,128)(2,1)S(1)} %get-tuple-element.14.p_v, f32[32,8192]{1,0:T(8,128)S(1)} %get-tuple-element.15.upd, f32[32,8192]{1,0:T(8,128)S(1)} %get-tuple-element.16.new1_v, ...), custom_call_target="tpu_custom_call" | custom-call | tf_op jit(solution)/shard_map/pallas_call | solution.py:421
